TPU v7x, 32 devices: a whole 2x2x4 slice. The times are simulated.
32 devices in a mesh: fsdp: 16 (over z, x, core), tp: 2 (over y).
Axes of the slice: x: 2, y: 2, z: 4, core: 2. Of those that a mesh axis runs over, the one named last changes fastest.
Arguments:
- saved_master: float32 [16384, 5120], P(('fsdp', 'tp')), may hold values from -6 to 6
- saved_first: float32 [16384, 5120], P(('fsdp', 'tp')), may hold values from -6 to 6
- saved_second: float32 [16384, 5120], P(('fsdp', 'tp')), may hold values from 0.05 to 20
- grad: bfloat16 [16384, 5120], P('fsdp', 'tp'), may hold values from -10000 to 10000
- row_target: int32 [16384], replicated, may hold values from 0 to 16383, as said below
- step: int32 [1], replicated, may hold values from 1 to 63
Outputs:
- new_master: float32 [16384, 5120], P('fsdp', 'tp')
- new_first: float32 [16384, 5120], P('fsdp', 'tp')
- new_second: float32 [16384, 5120], P('fsdp', 'tp')
- direction: float32 [16384, 5120], P('fsdp', 'tp')
Inputs may be any that keep to these rules, and one draw needn't show every extreme that they name: `row_target`: a permutation of 0 to 16383; the saved rows j * 1024 to (j + 1) * 1024 - 1 of every block j send exactly 64 rows into every new block of 1024 rows.
All inputs are finite; a program needn't handle non-finite values.
Results may differ from a plain program's by a relative error of at most 0.0003.
Values sent between devices are 32-bit elements; how exact they have to be, the bound alone decides.
No kernel may reach another device: no remote copies, remote signals or barrier semaphores. Data moves between devices by JAX's collectives and lax.ppermute only.
A program may use at most 192 MiB of HBM per device.

v0:
```python
import math

import jax
import jax.numpy as jnp
from jax import lax
from jax.sharding import PartitionSpec as P

H = 16384
D = 5120


beta_one = 0.9
beta_two = 0.95
epsilon = 1e-08
learn_rate = 0.001
weight_decay = 0.1


def adam_update(master, first, second, grad, scale, step):
    clipped = scale * grad.astype(jnp.float32)
    first_new = beta_one * first + (1.0 - beta_one) * clipped
    second_new = beta_two * second + (1.0 - beta_two) * clipped * clipped
    count = step[0].astype(jnp.float32)
    first_hat = first_new / (1.0 - jnp.power(jnp.float32(beta_one), count))
    second_hat = second_new / (1.0 - jnp.power(jnp.float32(beta_two), count))
    direction = first_hat / (jnp.sqrt(second_hat) + epsilon) + weight_decay * master
    return (master - learn_rate * direction, first_new, second_new, direction)


def per_device(saved_master, saved_first, saved_second, grad, row_target, step):
    tp_count = lax.axis_size("tp")
    fsdp_count = lax.axis_size("fsdp")
    block_index = lax.axis_index("fsdp")
    block_rows = grad.shape[0]
    all_rows = row_target.shape[0]
    grad_wide = grad.astype(jnp.float32)
    local_square = jnp.sum(grad_wide * grad_wide)
    mine = lax.dynamic_slice_in_dim(row_target, block_index * block_rows, block_rows)
    send_order = jnp.argsort(mine, stable=True)
    positions = jnp.arange(all_rows, dtype=jnp.int32)
    in_block = row_target // block_rows == block_index
    sort_keys = jnp.where(
        in_block, positions // block_rows * all_rows + row_target, all_rows * all_rows
    )
    picked = jnp.argsort(sort_keys, stable=True)[:block_rows]
    arrived_rows = row_target[picked] - block_index * block_rows
    place_order = jnp.argsort(arrived_rows, stable=True)
    tp_copies = jnp.full((1, tp_count), local_square, jnp.float32)
    middle = (
        lax.all_to_all(saved_master, "tp", split_axis=1, concat_axis=0, tiled=True),
        lax.all_to_all(saved_first, "tp", split_axis=1, concat_axis=0, tiled=True),
        lax.all_to_all(saved_second, "tp", split_axis=1, concat_axis=0, tiled=True),
        lax.all_to_all(tp_copies, "tp", split_axis=1, concat_axis=0, tiled=True),
    )
    row_square = jnp.sum(middle[3])
    fsdp_copies = jnp.full((fsdp_count, 1), row_square, jnp.float32)
    arrived = (
        lax.all_to_all(middle[0][send_order], "fsdp", split_axis=0, concat_axis=0, tiled=True),
        lax.all_to_all(middle[1][send_order], "fsdp", split_axis=0, concat_axis=0, tiled=True),
        lax.all_to_all(middle[2][send_order], "fsdp", split_axis=0, concat_axis=0, tiled=True),
        lax.all_to_all(fsdp_copies, "fsdp", split_axis=0, concat_axis=0, tiled=True),
    )
    total = jnp.sum(arrived[3])
    master = arrived[0][place_order]
    first = arrived[1][place_order]
    second = arrived[2][place_order]
    scale = jnp.minimum(1.0, math.sqrt(H * D) / jnp.sqrt(total))
    return adam_update(master, first, second, grad, scale, step)


def solution(mesh):
    in_specs = (
        P(("fsdp", "tp"), None),
        P(("fsdp", "tp"), None),
        P(("fsdp", "tp"), None),
        P("fsdp", "tp"),
        P(),
        P(),
    )
    out_specs = (P("fsdp", "tp"), P("fsdp", "tp"), P("fsdp", "tp"), P("fsdp", "tp"))
    return jax.shard_map(
        per_device, mesh=mesh, in_specs=in_specs, out_specs=out_specs, check_vma=False
    )
```

profile of v0, /device:TPU:11, one launch (start us, length us, event | category | flops | bytes accessed | tf_op | source)
XLA Modules:
  0.0 1137.6 jit_solution(8352183307849591315)
XLA Ops:
  0.6 5.8 fusion.2
  6.4 0.6 broadcast_in_dim.27
  7.1 5.0 all_to_all.109
  12.0 0.6 reduce_sum.28
  12.6 1.2 broadcast_in_dim.28
  13.9 7.9 all-to-all-start.5
  21.8 8.9 copy.34
  30.7 0.0 all-to-all-done.5
  30.7 7.7 all-to-all-start.2
  38.4 8.9 copy.33
  47.4 105.6 %all-to-all-done.2 = f32[512,2,2560]{2,0,1:T(8,128)} async-done(((f32[512,2,2560]{2,0,1:T(8,128)}), f32[512,2,2560]{2,0,1:T(8,128)}, u32[]{:S(2)}, u32[]{:S(2)}) %all-to-all-start.2) | async-done | bytes 10485792 | tf_op jit(solution)/shard_map/all_to_all | solution.py:51
  152.9 7.7 all-to-all-start.6
  160.7 8.9 copy.35
  169.6 104.7 %all-to-all-done.6 = f32[512,2,2560]{2,0,1:T(8,128)} async-done(((f32[512,2,2560]{2,0,1:T(8,128)}), f32[512,2,2560]{2,0,1:T(8,128)}, u32[]{:S(2)}, u32[]{:S(2)}) %all-to-all-start.6) | async-done | bytes 10485792 | tf_op jit(solution)/shard_map/all_to_all | solution.py:52
  274.3 0.0 copy-start
  274.3 7.8 all-to-all-start
  282.2 0.0 copy-done
  282.2 4.4 sort.48
  286.6 14.2 %gather_fusion.3 = f32[1024,2560]{1,0:T(8,128)} fusion(f32[1024,2560]{1,0:T(8,128)} %bitcast.5, s32[1024]{0:T(1024)S(1)} %fusion.13), kind=kCustom, calls=%fused_computation.3 | custom fusion | bytes 20975616 | tf_op jit(solution)/shard_map/gather | solution.py:59
  300.8 94.1 %all-to-all-done = f32[512,2,2560]{2,0,1:T(8,128)} async-done(((f32[512,2,2560]{2,0,1:T(8,128)}), f32[512,2,2560]{2,0,1:T(8,128)}, u32[]{:S(2)}, u32[]{:S(2)}) %all-to-all-start) | async-done | bytes 10485792 | tf_op jit(solution)/shard_map/all_to_all | solution.py:50
  394.9 8.6 all-to-all-start.3
  403.5 14.2 %gather_fusion.5 = f32[1024,2560]{1,0:T(8,128)} fusion(f32[1024,2560]{1,0:T(8,128)} %bitcast.10, s32[1024]{0:T(1024)S(1)} %fusion.13), kind=kCustom, calls=%fused_computation.5 | custom fusion | bytes 20975616 | tf_op jit(solution)/shard_map/gather | solution.py:60
  417.8 213.1 %all-to-all-done.3 = f32[16,64,2560]{2,1,0:T(8,128)} async-done(((f32[16,64,2560]{2,1,0:T(8,128)}), f32[16,64,2560]{2,1,0:T(8,128)}, u32[]{:S(2)}, u32[]{:S(2)}) %all-to-all-start.3) | async-done | bytes 10485792 | tf_op jit(solution)/shard_map/all_to_all | solution.py:59
  630.8 4.8 all-to-all-start.7
  635.6 14.2 %gather_fusion = f32[1024,2560]{1,0:T(8,128)} fusion(f32[1024,2560]{1,0:T(8,128)} %bitcast.1, s32[1024]{0:T(1024)S(1)} %fusion.13), kind=kCustom, calls=%fused_computation | custom fusion | bytes 20975616 | tf_op jit(solution)/shard_map/gather | solution.py:58
  649.8 213.1 %all-to-all-done.7 = f32[16,64,2560]{2,1,0:T(8,128)} async-done(((f32[16,64,2560]{2,1,0:T(8,128)}), f32[16,64,2560]{2,1,0:T(8,128)}, u32[]{:S(2)}, u32[]{:S(2)}) %all-to-all-start.7) | async-done | bytes 10485792 | tf_op jit(solution)/shard_map/all_to_all | solution.py:60
  862.9 5.0 all-to-all-start.1
  867.9 0.1 fusion.8
  868.0 7.8 sort.49
  875.7 6.1 gather_fusion.1
  882.6 4.4 sort.50
  887.0 0.6 reduce_sum.29
  888.3 14.2 %gather_fusion.4 = f32[1024,2560]{1,0:T(8,128)} fusion(f32[1024,2560]{1,0:T(8,128)} %bitcast.7, s32[1024]{0:T(1024)S(1)} %fusion.15), kind=kCustom, calls=%fused_computation.4 | custom fusion | bytes 20975616 | tf_op jit(solution)/shard_map/gather | solution.py:65
  902.5 14.2 %gather_fusion.6 = f32[1024,2560]{1,0:T(8,128)} fusion(f32[1024,2560]{1,0:T(8,128)} %bitcast.12, s32[1024]{0:T(1024)S(1)} %fusion.15), kind=kCustom, calls=%fused_computation.6 | custom fusion | bytes 20975616 | tf_op jit(solution)/shard_map/gather | solution.py:66
  916.8 178.2 %all-to-all-done.1 = f32[16,64,2560]{2,1,0:T(8,128)} async-done(((f32[16,64,2560]{2,1,0:T(8,128)}), f32[16,64,2560]{2,1,0:T(8,128)}, u32[]{:S(2)}, u32[]{:S(2)}) %all-to-all-start.1) | async-done | bytes 10485792 | tf_op jit(solution)/shard_map/all_to_all | solution.py:58
  1095.0 14.2 %gather_fusion.2 = f32[1024,2560]{1,0:T(8,128)} fusion(f32[1024,2560]{1,0:T(8,128)} %bitcast.3, s32[1024]{0:T(1024)S(1)} %fusion.15), kind=kCustom, calls=%fused_computation.2 | custom fusion | bytes 20975616 | tf_op jit(solution)/shard_map/gather | solution.py:64
  1109.2 28.4 %multiply_subtract_fusion = (f32[1024,2560]{1,0:T(8,128)}, f32[1024,2560]{1,0:T(8,128)}, f32[1024,2560]{1,0:T(8,128)}, f32[1024,2560]{1,0:T(8,128)}) fusion(f32[1024,2560]{1,0:T(8,128)} %gather_fusion.2, f32[]{:T(128)} %bitcast.13, f32[]{:T(128)} %bitcast.8, bf16[1024,2560]{1,0:T(8,128)(2,1)} %param.9, f32[]{:T(128)S(6)} %min.3, ...), kind=kLoop, calls=%fused_computation.17 | loop fusion | flops 44564480 | bytes 78643216 | tf_op jit(solution)/shard_map/sub | solution.py:27
  (8 shorter events, 0.0 us)
Async XLA Ops:
  13.9 16.9 %all-to-all-start.5 = ((f32[16,1,1]{2,1,0:T(1,128)}), f32[16,1,1]{2,1,0:T(1,128)S(1)}, u32[]{:S(2)}, u32[]{:S(2)}) async-start(f32[16,1,1]{2,1,0:T(1,128)} %broadcast_in_dim.28), calls=%async_computation.5 | async-start | bytes 16384 | tf_op jit(solution)/shard_map/all_to_all | solution.py:61
  30.7 122.2 %all-to-all-start.2 = ((f32[512,2,2560]{2,0,1:T(8,128)}), f32[512,2,2560]{2,0,1:T(8,128)}, u32[]{:S(2)}, u32[]{:S(2)}) async-start(f32[512,2,2560]{2,0,1:T(8,128)} %bitcast.33), calls=%async_computation.2 | async-start | bytes 20971520 | tf_op jit(solution)/shard_map/all_to_all | solution.py:51
  152.9 121.4 %all-to-all-start.6 = ((f32[512,2,2560]{2,0,1:T(8,128)}), f32[512,2,2560]{2,0,1:T(8,128)}, u32[]{:S(2)}, u32[]{:S(2)}) async-start(f32[512,2,2560]{2,0,1:T(8,128)} %bitcast.34), calls=%async_computation.6 | async-start | bytes 20971520 | tf_op jit(solution)/shard_map/all_to_all | solution.py:52
  274.3 7.8 copy-start
  274.3 120.6 %all-to-all-start = ((f32[512,2,2560]{2,0,1:T(8,128)}), f32[512,2,2560]{2,0,1:T(8,128)}, u32[]{:S(2)}, u32[]{:S(2)}) async-start(f32[512,2,2560]{2,0,1:T(8,128)} %bitcast.32), calls=%async_computation | async-start | bytes 20971520 | tf_op jit(solution)/shard_map/all_to_all | solution.py:50
  394.9 235.9 %all-to-all-start.3 = ((f32[16,64,2560]{2,1,0:T(8,128)}), f32[16,64,2560]{2,1,0:T(8,128)}, u32[]{:S(2)}, u32[]{:S(2)}) async-start(f32[16,64,2560]{2,1,0:T(8,128)} %bitcast.31), calls=%async_computation.3 | async-start | bytes 20971520 | tf_op jit(solution)/shard_map/all_to_all | solution.py:59
  630.8 232.1 %all-to-all-start.7 = ((f32[16,64,2560]{2,1,0:T(8,128)}), f32[16,64,2560]{2,1,0:T(8,128)}, u32[]{:S(2)}, u32[]{:S(2)}) async-start(f32[16,64,2560]{2,1,0:T(8,128)} %bitcast.30), calls=%async_computation.7 | async-start | bytes 20971520 | tf_op jit(solution)/shard_map/all_to_all | solution.py:60
  862.9 232.1 %all-to-all-start.1 = ((f32[16,64,2560]{2,1,0:T(8,128)}), f32[16,64,2560]{2,1,0:T(8,128)}, u32[]{:S(2)}, u32[]{:S(2)}) async-start(f32[16,64,2560]{2,1,0:T(8,128)} %bitcast.29), calls=%async_computation.1 | async-start | bytes 20971520 | tf_op jit(solution)/shard_map/all_to_all | solution.py:58
where the time goes:
time: 1140 us
  waiting for transfers between devices  909 us (80%)
  local copies, waits for them, and re-layouts  120 us (11%)
  other arithmetic  51.9 us (5%)
  starting transfers between devices  49.5 us (4%)
    all_to_all x1, waiting for transfers between devices, per_device(): lax.all_to_all(middle[1][send_order], 'fsdp', split_axis=0, concat_axis=0...  213 us
    all_to_all x1, waiting for transfers between devices, per_device(): lax.all_to_all(middle[2][send_order], 'fsdp', split_axis=0, concat_axis=0...  213 us
    all_to_all x1, waiting for transfers between devices, per_device(): lax.all_to_all(middle[0][send_order], 'fsdp', split_axis=0, concat_axis=0...  178 us
    all_to_all x1, waiting for transfers between devices, per_device(): lax.all_to_all(saved_first, 'tp', split_axis=1, concat_axis=0, tiled=True)  106 us
    all_to_all x1, waiting for transfers between devices, per_device(): lax.all_to_all(saved_second, 'tp', split_axis=1, concat_axis=0, tiled=True)  105 us
    all_to_all x1, waiting for transfers between devices, per_device(): lax.all_to_all(saved_master, 'tp', split_axis=1, concat_axis=0, tiled=True)  94.1 us
    sub x1, other arithmetic, adam_update(): return (master - learn_rate * direction, first_new, second_new, direction)  28.4 us
  transfers between devices with their start and end apart: 7, of which 6 were waited for; matrix products, arithmetic and copies ran while one was open for 11% of the time, Pallas kernels for 0%

commit v1 on v0

v1 whole, which is shorter than its diff:
```python
import math

import jax
import jax.numpy as jnp
from jax import lax
from jax.sharding import PartitionSpec as P


beta_one = 0.9
beta_two = 0.95
epsilon = 1e-08
learn_rate = 0.001
weight_decay = 0.1
lanes = 128
early_shares = (0.2, 0.3, 0.5)
late_shares = (0.75, 0.25)


def column_cuts(columns, shares):
    units = max(columns // lanes, 1)
    edges = {0, columns}
    total = 0.0
    for share in shares[:-1]:
        total += share
        edges.add(min(max(round(total * units), 1), units - 1) * (columns // units))
    edges = sorted(edges)
    return list(zip(edges[:-1], edges[1:]))


def after(value, *others):
    return lax.optimization_barrier((value,) + others)[0]


def per_device(saved_master, saved_first, saved_second, grad, row_target, step):
    tp_count = lax.axis_size("tp")
    block_index = lax.axis_index("fsdp")
    tp_index = lax.axis_index("tp")
    block_rows, columns = grad.shape
    piece_rows = saved_master.shape[0]
    all_rows = row_target.shape[0]

    mine = lax.dynamic_slice_in_dim(row_target, block_index * block_rows, block_rows)
    send_order = jnp.argsort(mine, stable=True)
    piece = (tp_index - send_order // piece_rows) % tp_count
    send_order = piece * piece_rows + send_order % piece_rows

    def tp_start(saved, low, high, wait_for=None):
        parts = []
        for shift in range(1, tp_count):
            target = (tp_index + shift) % tp_count
            out = lax.dynamic_slice(saved, (0, target * columns + low), (piece_rows, high - low))
            if wait_for is not None:
                out = after(out, wait_for)
            ring = [(i, (i + shift) % tp_count) for i in range(tp_count)]
            parts.append(lax.ppermute(out, "tp", ring))
        return parts

    def rows_to_send(saved, low, high, parts):
        own = lax.dynamic_slice(saved, (0, tp_index * columns + low), (piece_rows, high - low))
        return jnp.concatenate([own] + parts, axis=0)[send_order]

    def exchange(rows):
        return lax.all_to_all(rows, "fsdp", split_axis=0, concat_axis=0, tiled=True)

    jobs = [("second", low, high) for low, high in column_cuts(columns, early_shares)]
    jobs += [("first", 0, columns)]
    jobs += [("master", low, high) for low, high in column_cuts(columns, late_shares)]
    saved = {"master": saved_master, "first": saved_first, "second": saved_second}

    lead = tp_start(saved[jobs[0][0]], *jobs[0][1:])
    grad_wide = grad.astype(jnp.float32)
    local_square = jnp.sum(grad_wide * grad_wide)
    total = lax.psum(local_square, ("fsdp", "tp"))
    scale = jnp.minimum(1.0, math.sqrt(all_rows * saved_master.shape[1]) / jnp.sqrt(total))

    parts = [lead] + [
        tp_start(saved[name], low, high, total)
        for job, (name, low, high) in enumerate(jobs)
        if job > 0
    ]
    arrived = {}
    previous = total
    for job, (name, low, high) in enumerate(jobs):
        rows = rows_to_send(saved[name], low, high, parts[job])
        rows = after(rows, previous)
        previous = exchange(rows)
        arrived.setdefault(name, []).append((low, high, previous))

    positions = jnp.arange(all_rows, dtype=jnp.int32)
    in_block = row_target // block_rows == block_index
    sort_keys = jnp.where(
        in_block, positions // block_rows * all_rows + row_target, all_rows * all_rows
    )
    picked = jnp.argsort(sort_keys, stable=True)[:block_rows]
    arrived_rows = row_target[picked] - block_index * block_rows
    place_order = jnp.argsort(arrived_rows, stable=True)

    def placed(name):
        return jnp.concatenate([rows[place_order] for _, _, rows in arrived[name]], axis=1)

    count = step[0].astype(jnp.float32)
    clipped = scale * grad.astype(jnp.float32)
    first_new = beta_one * placed("first") + (1.0 - beta_one) * clipped
    second_new = beta_two * placed("second") + (1.0 - beta_two) * clipped * clipped
    first_hat = first_new / (1.0 - jnp.power(jnp.float32(beta_one), count))
    second_hat = second_new / (1.0 - jnp.power(jnp.float32(beta_two), count))
    update = first_hat / (jnp.sqrt(second_hat) + epsilon)
    direction = None
    for low, high, rows in arrived["master"]:
        master = rows[place_order]
        part = update[:, low:high] + weight_decay * master
        moved = master - learn_rate * part
        if direction is None:
            rest = ((0, 0), (low, columns - high))
            direction, new_master = lax.optimization_barrier(
                (jnp.pad(part, rest), jnp.pad(moved, rest))
            )
        else:
            direction = lax.dynamic_update_slice(direction, part, (0, low))
            new_master = lax.dynamic_update_slice(new_master, moved, (0, low))
    return new_master, first_new, second_new, direction


def solution(mesh):
    in_specs = (
        P(("fsdp", "tp"), None),
        P(("fsdp", "tp"), None),
        P(("fsdp", "tp"), None),
        P("fsdp", "tp"),
        P(),
        P(),
    )
    out_specs = (P("fsdp", "tp"), P("fsdp", "tp"), P("fsdp", "tp"), P("fsdp", "tp"))
    return jax.shard_map(
        per_device, mesh=mesh, in_specs=in_specs, out_specs=out_specs, check_vma=False
    )
```

time: 1140 us -> 841 us (0.74)
  waiting for transfers between devices: 909 us -> 522 us
  blocking collectives: 4.95 us -> 50.4 us
  local copies, waits for them, and re-layouts: 120 us -> 145 us
  other arithmetic: 51.9 us -> 76.2 us
    all_to_all x7 -> x6, waiting for transfers between devices: 909 us -> 224 us  [exchange(): return lax.all_to_all(rows, 'fsdp', split_axis=0, concat_axis=0, tiled=True)]
    ppermute x0 -> x6, waiting for transfers between devices: none -> 298 us  [tp_start(): parts.append(lax.ppermute(out, 'tp', ring))]
    psum x0 -> x1, blocking collectives: none -> 50.4 us  [per_device(): total = lax.psum(local_square, ('fsdp', 'tp'))]
    all_to_all x3 -> x0, local copies, waits for them, and re-layouts: 26.8 us -> none  [the longest x1 8.93 us: per_device(): lax.all_to_all(saved_second, 'tp', split_axis=1, concat_axis=0, tiled=True)]
    sub x1, other arithmetic: 28.4 us -> 6.24 us  [per_device(): moved = master - learn_rate * part]
    div x0 -> x1, other arithmetic: none -> 22 us  [per_device(): update = first_hat / (jnp.sqrt(second_hat) + epsilon)]
    dynamic_slice x0 -> x6, local copies, waits for them, and re-layouts: none -> 21 us  [rows_to_send(): lax.dynamic_slice(saved, (0, tp_index * columns + low), (piece_rows, high...]
    gather x6 -> x12, local copies, waits for them, and re-layouts: 85.4 us -> 106 us  [the longest x6 52.9 us: rows_to_send(): return jnp.concatenate([own] + parts, axis=0)[send_order]]
  transfers between devices with their start and end apart: 7 -> 12, of which waited for: 6 -> 9; matrix products, arithmetic and copies ran while one was open for 11% -> 24% of each run, Pallas kernels for 0% -> 0%
where the time goes in v1:
time: 841 us; the launch traced here: 840 us
  waiting for transfers between devices  522 us (62%)
  local copies, waits for them, and re-layouts  145 us (17%)
  other arithmetic  76.2 us (9%)
  blocking collectives  50.4 us (6%)
  starting transfers between devices  44.6 us (5%)
    ppermute x6, waiting for transfers between devices, tp_start(): parts.append(lax.ppermute(out, 'tp', ring))  298 us
    all_to_all x6, waiting for transfers between devices, exchange(): return lax.all_to_all(rows, 'fsdp', split_axis=0, concat_axis=0, tiled=True)  224 us
    gather x6, local copies, waits for them, and re-layouts, rows_to_send(): return jnp.concatenate([own] + parts, axis=0)[send_order]  52.9 us
    psum x1, blocking collectives, per_device(): total = lax.psum(local_square, ('fsdp', 'tp'))  50.4 us
    gather x4, local copies, waits for them, and re-layouts, placed(): rows[place_order]  35.8 us
    all_to_all x6, starting transfers between devices, exchange(): return lax.all_to_all(rows, 'fsdp', split_axis=0, concat_axis=0, tiled=True)  35 us
    div x1, other arithmetic, per_device(): update = first_hat / (jnp.sqrt(second_hat) + epsilon)  22 us
    dynamic_slice x6, local copies, waits for them, and re-layouts, rows_to_send(): lax.dynamic_slice(saved, (0, tp_index * columns + low), (piece_rows, high...  21 us
  transfers between devices with their start and end apart: 12, of which 9 were waited for; matrix products, arithmetic and copies ran while one was open for 24% of the time, Pallas kernels for 0%

profile of v1, /device:TPU:11, one launch (start us, length us, event | category | flops | bytes accessed | tf_op | source)
XLA Modules:
  0.0 839.9 jit_solution(17277001439626934615)
XLA Ops:
  3.7 5.8 fusion.2
  9.5 50.4 %psum.7 = f32[]{:T(128)} all-reduce(f32[]{:T(128)} %fusion.2), channel_id=1, replica_groups=mesh['fsdp'=16,'tp'=2] {'fsdp','tp'}, use_global_device_ids=true, to_apply=%region_1.2 | all-reduce | flops 1 | bytes 8 | tf_op jit(solution)/shard_map/psum | solution.py:73
  59.9 4.4 sort.48
  66.7 4.9 gather_fusion.3
  71.5 7.2 all-to-all-start
  78.7 2.1 constant_dynamic-slice_fusion.7
  80.8 1.9 collective-permute-start.2
  82.7 34.4 %collective-permute-done.2 = f32[512,768]{1,0:T(8,128)S(1)} collective-permute-done((f32[512,768]{1,0:T(8,128)S(1)}, f32[512,768]{1,0:T(8,128)S(1)}, u32[]{:S(2)}, u32[]{:S(2)}) %collective-permute-start.2) | collective-permute-done | bytes 1572896 | tf_op jit(solution)/shard_map/ppermute | solution.py:55
  117.3 5.2 gather_fusion.2
  122.5 3.7 all-to-all-done
  126.3 4.8 all-to-all-start.1
  131.0 2.9 constant_dynamic-slice_fusion.9
  135.8 56.8 %collective-permute-done.1 = f32[512,1280]{1,0:T(8,128)S(1)} collective-permute-done((f32[512,1280]{1,0:T(8,128)S(1)}, f32[512,1280]{1,0:T(8,128)S(1)}, u32[]{:S(2)}, u32[]{:S(2)}) %collective-permute-start.1) | collective-permute-done | bytes 2621472 | tf_op jit(solution)/shard_map/ppermute | solution.py:55
  192.7 2.7 pad_maximum_fusion.2
  195.4 9.4 %gather_fusion.1 = f32[1024,1280]{1,0:T(8,128)} fusion(f32[1024,1280]{1,0:T(8,128)} %pad_maximum_fusion.2, s32[1024]{0:T(1024)S(1)} %fusion.18), kind=kCustom, calls=%fused_computation.1 | custom fusion | bytes 10489856 | tf_op jit(solution)/shard_map/gather | solution.py:60
  204.8 6.6 all-to-all-start.2
  211.4 7.1 constant_dynamic-slice_fusion.11
  220.0 112.9 %collective-permute-done = f32[512,2560]{1,0:T(8,128)} collective-permute-done((f32[512,2560]{1,0:T(8,128)S(1)}, f32[512,2560]{1,0:T(8,128)}, u32[]{:S(2)}, u32[]{:S(2)}) %collective-permute-start) | collective-permute-done | bytes 5242912 | tf_op jit(solution)/shard_map/ppermute | solution.py:55
  332.8 8.9 %pad_maximum_fusion = f32[1024,2560]{1,0:T(8,128)} fusion(f32[512,2560]{1,0:T(8,128)} %collective-permute-done, f32[512,2560]{1,0:T(8,128)} %get-tuple-element.47), kind=kLoop, calls=%fused_computation.20 | loop fusion | flops 2621440 | bytes 20971520 | tf_op jit(solution)/shard_map/concatenate | solution.py:60
  341.7 14.2 %gather_fusion = f32[1024,2560]{1,0:T(8,128)} fusion(f32[1024,2560]{1,0:T(8,128)} %pad_maximum_fusion, s32[1024]{0:T(1024)S(1)} %fusion.18), kind=kCustom, calls=%fused_computation | custom fusion | bytes 20975616 | tf_op jit(solution)/shard_map/gather | solution.py:60
  355.9 6.9 all-to-all-start.3
  362.8 3.8 constant_dynamic-slice_fusion.3
  368.2 84.8 %collective-permute-done.4 = f32[512,1920]{1,0:T(8,128)S(1)} collective-permute-done((f32[512,1920]{1,0:T(8,128)S(1)}, f32[512,1920]{1,0:T(8,128)S(1)}, u32[]{:S(2)}, u32[]{:S(2)}) %collective-permute-start.4) | collective-permute-done | bytes 3932192 | tf_op jit(solution)/shard_map/ppermute | solution.py:55
  452.9 3.7 pad_maximum_fusion.1
  456.6 11.8 %gather_fusion.9 = f32[1024,1920]{1,0:T(8,128)} fusion(f32[1024,1920]{1,0:T(8,128)} %pad_maximum_fusion.1, s32[1024]{0:T(1024)S(1)} %fusion.18), kind=kCustom, calls=%fused_computation.9 | custom fusion | bytes 15732736 | tf_op jit(solution)/shard_map/gather | solution.py:60
  468.5 121.6 %all-to-all-done.3 = f32[16,64,2560]{2,1,0:T(8,128)} async-done(((f32[16,64,2560]{2,1,0:T(8,128)}), f32[16,64,2560]{2,1,0:T(8,128)}, u32[]{:S(2)}, u32[]{:S(2)}) %all-to-all-start.3) | async-done | bytes 10485792 | tf_op jit(solution)/shard_map/all_to_all | solution.py:63
  590.1 4.8 all-to-all-start.4
  594.9 3.4 constant_dynamic-slice_fusion.1
  601.3 7.8 sort.49
  609.0 6.1 gather_fusion.4
  615.2 4.4 sort.50
  619.6 9.0 %collective-permute-done.5 = f32[512,640]{1,0:T(8,128)} collective-permute-done((f32[512,640]{1,0:T(8,128)}, f32[512,640]{1,0:T(8,128)}, u32[]{:S(2)}, u32[]{:S(2)}) %collective-permute-start.5) | collective-permute-done | bytes 1310752 | tf_op jit(solution)/shard_map/ppermute | solution.py:55
  628.6 3.4 pad_maximum_fusion.4
  632.0 7.3 gather_fusion.11
  639.3 6.9 gather_fusion.6
  646.1 5.3 gather_fusion.7
  651.4 9.4 %gather_fusion.8 = f32[1024,1280]{1,0:T(8,128)} fusion(f32[1024,1280]{1,0:T(8,128)} %bitcast.5, s32[1024]{0:T(1024)S(1)} %fusion.20), kind=kCustom, calls=%fused_computation.8 | custom fusion | bytes 10489856 | tf_op jit(solution)/shard_map/gather | solution.py:99
  660.9 14.2 %gather_fusion.5 = f32[1024,2560]{1,0:T(8,128)} fusion(f32[1024,2560]{1,0:T(8,128)} %bitcast.7, s32[1024]{0:T(1024)S(1)} %fusion.20), kind=kCustom, calls=%fused_computation.5 | custom fusion | bytes 20975616 | tf_op jit(solution)/shard_map/gather | solution.py:99
  675.1 90.9 %all-to-all-done.4 = f32[16,64,1920]{2,1,0:T(8,128)} async-done(((f32[16,64,1920]{2,1,0:T(8,128)}), f32[16,64,1920]{2,1,0:T(8,128)}, u32[]{:S(2)}, u32[]{:S(2)}) %all-to-all-start.4) | async-done | bytes 7864352 | tf_op jit(solution)/shard_map/all_to_all | solution.py:63
  766.0 4.8 all-to-all-start.5
  770.8 22.0 %multiply_divide_fusion = (f32[1024,2560]{1,0:T(8,128)}, f32[1024,2560]{1,0:T(8,128)}, f32[1024,2560]{1,0:T(8,128)}) fusion(f32[]{:T(128)} %bitcast.9, f32[]{:T(128)} %bitcast.8, bf16[1024,2560]{1,0:T(8,128)(2,1)} %param.9, f32[]{:T(128)S(6)} %min.3, f32[1024,1280]{1,0:T(8,128)} %gather_fusion.8, f32[1024,768]{1,0:T(8,128)} %gather_fusion.7, ...), kind=kLoop, calls=%fused_computation.22 | loop fusion | flops 39321600 | bytes 57671692 | tf_op jit(solution)/shard_map/div | solution.py:107
  792.7 11.8 %gather_fusion.10 = f32[1024,1920]{1,0:T(8,128)} fusion(f32[1024,1920]{1,0:T(8,128)} %bitcast.11, s32[1024]{0:T(1024)S(1)} %fusion.20), kind=kCustom, calls=%fused_computation.10 | custom fusion | bytes 15732736 | tf_op jit(solution)/shard_map/gather | solution.py:110
  804.6 6.2 multiply_subtract_fusion
  810.8 5.5 pad.8
  816.3 5.5 pad.7
  821.8 7.6 all-to-all-done.5
  829.4 5.2 gather_fusion.12
  834.6 5.3 fusion.4
  (24 shorter events, 12.1 us)
Async XLA Ops:
  0.6 59.2 %copy-start = (s32[16384]{0:T(1024)S(1)}, s32[16384]{0:T(1024)}, u32[]{:S(2)}) copy-start(s32[16384]{0:T(1024)} %param.10) | copy-start | bytes 196612
  2.4 61.9 %collective-permute-start.3 = (f32[512,512]{1,0:T(8,128)S(1)}, f32[512,512]{1,0:T(8,128)S(1)}, u32[]{:S(2)}, u32[]{:S(2)}) collective-permute-start(f32[512,512]{1,0:T(8,128)S(1)} %get-tuple-element.50), channel_id=1, source_target_pairs={{0,1},{1,0},{2,3},{3,2},{4,5},{5,4},{6,7},{7,6},{8,9},{9,8},{10,11... | collective-permute-start | bytes 3145736 | tf_op jit(solution)/shard_map/ppermute | solution.py:55
  64.3 1.0 copy-start.1
  71.5 54.7 %all-to-all-start = ((f32[16,64,512]{2,1,0:T(8,128)}), f32[16,64,512]{2,1,0:T(8,128)}, u32[]{:S(2)}, u32[]{:S(2)}) async-start(f32[16,64,512]{2,1,0:T(8,128)} %bitcast.21), calls=%async_computation | async-start | bytes 4194304 | tf_op jit(solution)/shard_map/all_to_all | solution.py:63
  80.8 36.3 %collective-permute-start.2 = (f32[512,768]{1,0:T(8,128)S(1)}, f32[512,768]{1,0:T(8,128)S(1)}, u32[]{:S(2)}, u32[]{:S(2)}) collective-permute-start(f32[512,768]{1,0:T(8,128)S(1)} %get-tuple-element.23), channel_id=1, source_target_pairs={{0,1},{1,0},{2,3},{3,2},{4,5},{5,4},{6,7},{7,6},{8,9},{9,8},{10,11... | collective-permute-start | bytes 4718600 | tf_op jit(solution)/shard_map/ppermute | solution.py:55
  126.3 78.5 %all-to-all-start.1 = ((f32[16,64,768]{2,1,0:T(8,128)}), f32[16,64,768]{2,1,0:T(8,128)S(1)}, u32[]{:S(2)}, u32[]{:S(2)}) async-start(f32[16,64,768]{2,1,0:T(8,128)} %bitcast.19), calls=%async_computation.1 | async-start | bytes 6291456 | tf_op jit(solution)/shard_map/all_to_all | solution.py:63
  133.9 58.8 %collective-permute-start.1 = (f32[512,1280]{1,0:T(8,128)S(1)}, f32[512,1280]{1,0:T(8,128)S(1)}, u32[]{:S(2)}, u32[]{:S(2)}) collective-permute-start(f32[512,1280]{1,0:T(8,128)S(1)} %get-tuple-element.22), channel_id=1, source_target_pairs={{0,1},{1,0},{2,3},{3,2},{4,5},{5,4},{6,7},{7,6},{8,9},{9,8},{10,11... | collective-permute-start | bytes 7864328 | tf_op jit(solution)/shard_map/ppermute | solution.py:55
  204.8 151.1 %all-to-all-start.2 = ((f32[16,64,1280]{2,1,0:T(8,128)}), f32[16,64,1280]{2,1,0:T(8,128)}, u32[]{:S(2)}, u32[]{:S(2)}) async-start(f32[16,64,1280]{2,1,0:T(8,128)} %bitcast.18), calls=%async_computation.2 | async-start | bytes 10485760 | tf_op jit(solution)/shard_map/all_to_all | solution.py:63
  218.5 114.3 %collective-permute-start = (f32[512,2560]{1,0:T(8,128)S(1)}, f32[512,2560]{1,0:T(8,128)}, u32[]{:S(2)}, u32[]{:S(2)}) collective-permute-start(f32[512,2560]{1,0:T(8,128)S(1)} %get-tuple-element.20), channel_id=1, source_target_pairs={{0,1},{1,0},{2,3},{3,2},{4,5},{5,4},{6,7},{7,6},{8,9},{9,8},{10,11... | collective-permute-start | bytes 15728648 | tf_op jit(solution)/shard_map/ppermute | solution.py:55
  355.9 234.2 %all-to-all-start.3 = ((f32[16,64,2560]{2,1,0:T(8,128)}), f32[16,64,2560]{2,1,0:T(8,128)}, u32[]{:S(2)}, u32[]{:S(2)}) async-start(f32[16,64,2560]{2,1,0:T(8,128)} %bitcast.16), calls=%async_computation.3 | async-start | bytes 20971520 | tf_op jit(solution)/shard_map/all_to_all | solution.py:63
  366.6 86.3 %collective-permute-start.4 = (f32[512,1920]{1,0:T(8,128)S(1)}, f32[512,1920]{1,0:T(8,128)S(1)}, u32[]{:S(2)}, u32[]{:S(2)}) collective-permute-start(f32[512,1920]{1,0:T(8,128)S(1)} %get-tuple-element.30), channel_id=1, source_target_pairs={{0,1},{1,0},{2,3},{3,2},{4,5},{5,4},{6,7},{7,6},{8,9},{9,8},{10,11... | collective-permute-start | bytes 11796488 | tf_op jit(solution)/shard_map/ppermute | solution.py:55
  590.1 175.9 %all-to-all-start.4 = ((f32[16,64,1920]{2,1,0:T(8,128)}), f32[16,64,1920]{2,1,0:T(8,128)}, u32[]{:S(2)}, u32[]{:S(2)}) async-start(f32[16,64,1920]{2,1,0:T(8,128)} %bitcast.17), calls=%async_computation.4 | async-start | bytes 15728640 | tf_op jit(solution)/shard_map/all_to_all | solution.py:63
  598.3 30.3 %collective-permute-start.5 = (f32[512,640]{1,0:T(8,128)}, f32[512,640]{1,0:T(8,128)}, u32[]{:S(2)}, u32[]{:S(2)}) collective-permute-start(f32[512,640]{1,0:T(8,128)} %get-tuple-element.33), channel_id=1, source_target_pairs={{0,1},{1,0},{2,3},{3,2},{4,5},{5,4},{6,7},{7,6},{8,9},{9,8},{10,11... | collective-permute-start | bytes 3932168 | tf_op jit(solution)/shard_map/ppermute | solution.py:55
  766.0 63.4 %all-to-all-start.5 = ((f32[16,64,640]{2,1,0:T(8,128)}), f32[16,64,640]{2,1,0:T(8,128)S(1)}, u32[]{:S(2)}, u32[]{:S(2)}) async-start(f32[16,64,640]{2,1,0:T(8,128)} %bitcast.20), calls=%async_computation.5 | async-start | bytes 5242880 | tf_op jit(solution)/shard_map/all_to_all | solution.py:63

commit v2 on v1

--- a/solution.py
+++ b/solution.py
@@ -13,7 +13,7 @@
 weight_decay = 0.1
 lanes = 128
 early_shares = (0.2, 0.3, 0.5)
-late_shares = (0.75, 0.25)
+late_shares = (0.8, 0.2)
 
 
 def column_cuts(columns, shares):
@@ -35,6 +35,7 @@
     tp_count = lax.axis_size("tp")
     block_index = lax.axis_index("fsdp")
     tp_index = lax.axis_index("tp")
+    fsdp_count = lax.axis_size("fsdp")
     block_rows, columns = grad.shape
     piece_rows = saved_master.shape[0]
     all_rows = row_target.shape[0]
@@ -44,13 +45,11 @@
     piece = (tp_index - send_order // piece_rows) % tp_count
     send_order = piece * piece_rows + send_order % piece_rows
 
-    def tp_start(saved, low, high, wait_for=None):
+    def tp_start(saved, low, high):
         parts = []
         for shift in range(1, tp_count):
             target = (tp_index + shift) % tp_count
             out = lax.dynamic_slice(saved, (0, target * columns + low), (piece_rows, high - low))
-            if wait_for is not None:
-                out = after(out, wait_for)
             ring = [(i, (i + shift) % tp_count) for i in range(tp_count)]
             parts.append(lax.ppermute(out, "tp", ring))
         return parts
@@ -67,24 +66,29 @@
     jobs += [("master", low, high) for low, high in column_cuts(columns, late_shares)]
     saved = {"master": saved_master, "first": saved_first, "second": saved_second}
 
-    lead = tp_start(saved[jobs[0][0]], *jobs[0][1:])
+    parts = [tp_start(saved[name], low, high) for name, low, high in jobs]
     grad_wide = grad.astype(jnp.float32)
     local_square = jnp.sum(grad_wide * grad_wide)
-    total = lax.psum(local_square, ("fsdp", "tp"))
+    copies = jnp.full((fsdp_count, 1), local_square, jnp.float32)
+    copies = lax.all_to_all(copies, "fsdp", split_axis=0, concat_axis=0, tiled=True)
+    column_square = jnp.sum(copies)
+    total = column_square
+    for shift in range(1, tp_count):
+        ring = [(i, (i + shift) % tp_count) for i in range(tp_count)]
+        total = total + lax.ppermute(column_square, "tp", ring)
     scale = jnp.minimum(1.0, math.sqrt(all_rows * saved_master.shape[1]) / jnp.sqrt(total))
 
-    parts = [lead] + [
-        tp_start(saved[name], low, high, total)
-        for job, (name, low, high) in enumerate(jobs)
-        if job > 0
-    ]
-    arrived = {}
-    previous = total
-    for job, (name, low, high) in enumerate(jobs):
-        rows = rows_to_send(saved[name], low, high, parts[job])
-        rows = after(rows, previous)
-        previous = exchange(rows)
-        arrived.setdefault(name, []).append((low, high, previous))
+    arrived = {"master": [], "first": [], "second": []}
+
+    def run(job, *previous):
+        name, low, high = jobs[job]
+        rows = after(rows_to_send(saved[name], low, high, parts[job]), *previous)
+        arrived[name].append((low, high, exchange(rows)))
+        return arrived[name][-1][2]
+
+    previous = column_square
+    for job in range(len(jobs) - 1):
+        previous = run(job, previous)
 
     positions = jnp.arange(all_rows, dtype=jnp.int32)
     in_block = row_target // block_rows == block_index
@@ -105,6 +109,7 @@
     first_hat = first_new / (1.0 - jnp.power(jnp.float32(beta_one), count))
     second_hat = second_new / (1.0 - jnp.power(jnp.float32(beta_two), count))
     update = first_hat / (jnp.sqrt(second_hat) + epsilon)
+    run(len(jobs) - 1, previous, update)
     direction = None
     for low, high, rows in arrived["master"]:
         master = rows[place_order]

time: 841 us -> 802 us (0.954)
  blocking collectives: 50.4 us -> 0 us
    psum x1 -> x0, blocking collectives: 50.4 us -> none  [per_device(): total = lax.psum(local_square, ('fsdp', 'tp'))]
    all_to_all x6, waiting for transfers between devices: 224 us -> 213 us  [exchange(): return lax.all_to_all(rows, 'fsdp', split_axis=0, concat_axis=0, tiled=True)]
  transfers between devices with their start and end apart: 12 -> 14, of which waited for: 9 -> 10; matrix products, arithmetic and copies ran while one was open for 24% -> 26% of each run, Pallas kernels for 0% -> 0%
where the time goes in v2:
time: 802 us; the launch traced here: 801 us
  waiting for transfers between devices  516 us (64%)
  local copies, waits for them, and re-layouts  151 us (19%)
  other arithmetic  81 us (10%)
  starting transfers between devices  50.2 us (6%)
    ppermute x6, waiting for transfers between devices, tp_start(): parts.append(lax.ppermute(out, 'tp', ring))  299 us
    all_to_all x6, waiting for transfers between devices, exchange(): return lax.all_to_all(rows, 'fsdp', split_axis=0, concat_axis=0, tiled=True)  213 us
    gather x6, local copies, waits for them, and re-layouts, rows_to_send(): return jnp.concatenate([own] + parts, axis=0)[send_order]  53 us
    gather x4, local copies, waits for them, and re-layouts, placed(): rows[place_order]  35.9 us
    all_to_all x6, starting transfers between devices, exchange(): return lax.all_to_all(rows, 'fsdp', split_axis=0, concat_axis=0, tiled=True)  35.5 us
    concatenate x6, other arithmetic, rows_to_send(): return jnp.concatenate([own] + parts, axis=0)[send_order]  22.8 us
    div x1, other arithmetic, per_device(): update = first_hat / (jnp.sqrt(second_hat) + epsilon)  20.9 us
    dynamic_slice x6, local copies, waits for them, and re-layouts, rows_to_send(): lax.dynamic_slice(saved, (0, tp_index * columns + low), (piece_rows, high...  20.9 us
  transfers between devices with their start and end apart: 14, of which 10 were waited for; matrix products, arithmetic and copies ran while one was open for 26% of the time, Pallas kernels for 0%

profile of v2, /device:TPU:11, one launch (start us, length us, event | category | flops | bytes accessed | tf_op | source)
XLA Modules:
  0.0 801.3 jit_solution(2516083110438210023)
XLA Ops:
  3.7 5.8 fusion.2
  10.7 6.8 all-to-all-start
  17.6 4.4 sort.48
  22.6 3.9 collective-permute-done.3
  28.9 4.9 gather_fusion.3
  33.7 7.4 all-to-all-start.1
  41.1 2.1 constant_dynamic-slice_fusion.7
  44.5 34.3 %collective-permute-done.2 = f32[512,768]{1,0:T(8,128)S(1)} collective-permute-done((f32[512,768]{1,0:T(8,128)S(1)}, f32[512,768]{1,0:T(8,128)S(1)}, u32[]{:S(2)}, u32[]{:S(2)}) %collective-permute-start.2) | collective-permute-done | bytes 1572896 | tf_op jit(solution)/shard_map/ppermute | solution.py:54
  79.0 5.2 gather_fusion.2
  84.3 4.4 all-to-all-done.1
  88.6 4.8 all-to-all-start.2
  93.4 2.9 constant_dynamic-slice_fusion.9
  97.6 56.8 %collective-permute-done.1 = f32[512,1280]{1,0:T(8,128)S(1)} collective-permute-done((f32[512,1280]{1,0:T(8,128)S(1)}, f32[512,1280]{1,0:T(8,128)S(1)}, u32[]{:S(2)}, u32[]{:S(2)}) %collective-permute-start.1) | collective-permute-done | bytes 2621472 | tf_op jit(solution)/shard_map/ppermute | solution.py:54
  154.4 2.7 pad_maximum_fusion.2
  157.1 9.4 %gather_fusion.1 = f32[1024,1280]{1,0:T(8,128)} fusion(f32[1024,1280]{1,0:T(8,128)} %pad_maximum_fusion.2, s32[1024]{0:T(1024)S(1)} %fusion.18), kind=kCustom, calls=%fused_computation.1 | custom fusion | bytes 10489856 | tf_op jit(solution)/shard_map/gather | solution.py:59
  166.5 6.9 all-to-all-start.3
  173.4 7.1 constant_dynamic-slice_fusion.11
  181.8 113.1 %collective-permute-done = f32[512,2560]{1,0:T(8,128)} collective-permute-done((f32[512,2560]{1,0:T(8,128)S(1)}, f32[512,2560]{1,0:T(8,128)}, u32[]{:S(2)}, u32[]{:S(2)}) %collective-permute-start) | collective-permute-done | bytes 5242912 | tf_op jit(solution)/shard_map/ppermute | solution.py:54
  294.8 8.9 %pad_maximum_fusion = f32[1024,2560]{1,0:T(8,128)} fusion(f32[512,2560]{1,0:T(8,128)} %collective-permute-done, f32[512,2560]{1,0:T(8,128)} %get-tuple-element.37), kind=kLoop, calls=%fused_computation.20 | loop fusion | flops 2621440 | bytes 20971520 | tf_op jit(solution)/shard_map/concatenate | solution.py:59
  303.7 14.2 %gather_fusion = f32[1024,2560]{1,0:T(8,128)} fusion(f32[1024,2560]{1,0:T(8,128)} %pad_maximum_fusion, s32[1024]{0:T(1024)S(1)} %fusion.18), kind=kCustom, calls=%fused_computation | custom fusion | bytes 20975616 | tf_op jit(solution)/shard_map/gather | solution.py:59
  317.9 6.9 all-to-all-start.4
  324.8 4.0 constant_dynamic-slice_fusion.3
  330.2 90.6 %collective-permute-done.5 = f32[512,2048]{1,0:T(8,128)S(1)} collective-permute-done((f32[512,2048]{1,0:T(8,128)S(1)}, f32[512,2048]{1,0:T(8,128)S(1)}, u32[]{:S(2)}, u32[]{:S(2)}) %collective-permute-start.5) | collective-permute-done | bytes 4194336 | tf_op jit(solution)/shard_map/ppermute | solution.py:54
  422.8 6.7 pad_maximum_fusion.1
  429.4 12.3 %gather_fusion.9 = f32[1024,2048]{1,0:T(8,128)} fusion(f32[1024,2048]{1,0:T(8,128)} %pad_maximum_fusion.1, s32[1024]{0:T(1024)S(1)} %fusion.18), kind=kCustom, calls=%fused_computation.9 | custom fusion | bytes 16781312 | tf_op jit(solution)/shard_map/gather | solution.py:59
  441.8 110.4 %all-to-all-done.4 = f32[16,64,2560]{2,1,0:T(8,128)} async-done(((f32[16,64,2560]{2,1,0:T(8,128)}), f32[16,64,2560]{2,1,0:T(8,128)}, u32[]{:S(2)}, u32[]{:S(2)}) %all-to-all-start.4) | async-done | bytes 10485792 | tf_op jit(solution)/shard_map/all_to_all | solution.py:62
  552.1 4.8 all-to-all-start.5
  556.9 3.0 constant_dynamic-slice_fusion.1
  562.0 7.8 sort.49
  569.8 6.1 gather_fusion.4
  576.0 4.4 sort.50
  580.6 4.1 collective-permute-done.4
  586.1 3.0 pad_maximum_fusion.5
  589.1 6.9 gather_fusion.11
  596.0 6.9 gather_fusion.6
  602.9 5.2 gather_fusion.7
  608.1 9.4 %gather_fusion.8 = f32[1024,1280]{1,0:T(8,128)} fusion(f32[1024,1280]{1,0:T(8,128)} %bitcast.5, s32[1024]{0:T(1024)S(1)} %fusion.20), kind=kCustom, calls=%fused_computation.8 | custom fusion | bytes 10489856 | tf_op jit(solution)/shard_map/gather | solution.py:103
  617.5 14.4 %gather_fusion.5 = f32[1024,2560]{1,0:T(8,128)} fusion(f32[1024,2560]{1,0:T(8,128)} %bitcast.7, s32[1024]{0:T(1024)S(1)} %fusion.20), kind=kCustom, calls=%fused_computation.5 | custom fusion | bytes 20975616 | tf_op jit(solution)/shard_map/gather | solution.py:103
  631.9 20.9 %multiply_divide_fusion = (f32[1024,2560]{1,0:T(8,128)}, f32[1024,2560]{1,0:T(8,128)}, f32[1024,2560]{1,0:T(8,128)}) fusion(f32[]{:T(128)} %bitcast.9, f32[]{:T(128)} %bitcast.8, bf16[1024,2560]{1,0:T(8,128)(2,1)} %param.9, f32[]{:T(128)S(6)} %min.3, f32[1024,1280]{1,0:T(8,128)} %gather_fusion.8, f32[1024,768]{1,0:T(8,128)S(1)} %copy-done.1, ...), kind=kLoop, calls=%fused_computation.22 | loop fusion | flops 39321600 | bytes 57671692 | tf_op jit(solution)/shard_map/div | solution.py:111
  652.9 86.4 %all-to-all-done.5 = f32[16,64,2048]{2,1,0:T(8,128)} async-done(((f32[16,64,2048]{2,1,0:T(8,128)}), f32[16,64,2048]{2,1,0:T(8,128)}, u32[]{:S(2)}, u32[]{:S(2)}) %all-to-all-start.5) | async-done | bytes 8388640 | tf_op jit(solution)/shard_map/all_to_all | solution.py:62
  739.2 4.8 all-to-all-start.6
  744.0 12.2 %gather_fusion.10 = f32[1024,2048]{1,0:T(8,128)} fusion(f32[1024,2048]{1,0:T(8,128)} %bitcast.11, s32[1024]{0:T(1024)S(1)} %fusion.20), kind=kCustom, calls=%fused_computation.10 | custom fusion | bytes 16781312 | tf_op jit(solution)/shard_map/gather | solution.py:115
  756.3 9.3 %multiply_subtract_fusion = (f32[1024,2048]{1,0:T(8,128)}, f32[1024,2048]{1,0:T(8,128)S(1)}) fusion(f32[1024,2048]{1,0:T(8,128)} %gather_fusion.10, f32[1024,2560]{1,0:T(8,128)} %get-tuple-element.26), kind=kLoop, calls=%fused_computation.25 | loop fusion | flops 8388608 | bytes 33554432 | tf_op jit(solution)/shard_map/sub | solution.py:117
  765.6 8.6 %pad.8 = f32[1024,2560]{1,0:T(8,128)} pad(f32[1024,2048]{1,0:T(8,128)} %get-tuple-element.29, f32[]{:T(128)} %constant.127.clone.1), padding=0_0x0_512 | pad | bytes 18874372 | tf_op jit(solution)/shard_map/jit(_pad)/pad | solution.py:121
  774.1 5.0 pad.7
  779.1 12.3 %all-to-all-done.6 = f32[16,64,512]{2,1,0:T(8,128)S(1)} async-done(((f32[16,64,512]{2,1,0:T(8,128)}), f32[16,64,512]{2,1,0:T(8,128)S(1)}, u32[]{:S(2)}, u32[]{:S(2)}) %all-to-all-start.6) | async-done | bytes 2097184 | tf_op jit(solution)/shard_map/all_to_all | solution.py:62
  791.4 4.9 gather_fusion.12
  796.3 4.9 fusion.4
  (33 shorter events, 16.2 us)
Async XLA Ops:
  0.6 16.9 %copy-start = (s32[16384]{0:T(1024)S(1)}, s32[16384]{0:T(1024)}, u32[]{:S(2)}) copy-start(s32[16384]{0:T(1024)} %param.10) | copy-start | bytes 196612
  2.4 24.1 %collective-permute-start.3 = (f32[512,512]{1,0:T(8,128)S(1)}, f32[512,512]{1,0:T(8,128)S(1)}, u32[]{:S(2)}, u32[]{:S(2)}) collective-permute-start(f32[512,512]{1,0:T(8,128)S(1)} %get-tuple-element.40), channel_id=1, source_target_pairs={{0,1},{1,0},{2,3},{3,2},{4,5},{5,4},{6,7},{7,6},{8,9},{9,8},{10,11... | collective-permute-start | bytes 3145736 | tf_op jit(solution)/shard_map/ppermute | solution.py:54
  10.7 11.2 %all-to-all-start = ((f32[16,1,1]{2,1,0:T(1,128)}), f32[16,1,1]{2,1,0:T(1,128)S(1)}, u32[]{:S(2)}, u32[]{:S(2)}) async-start(f32[16,1,1]{2,1,0:T(1,128)} %broadcast_in_dim.13), calls=%async_computation | async-start | bytes 16384 | tf_op jit(solution)/shard_map/all_to_all | solution.py:73
  26.5 1.0 copy-start.3
  33.7 54.9 %all-to-all-start.1 = ((f32[16,64,512]{2,1,0:T(8,128)}), f32[16,64,512]{2,1,0:T(8,128)}, u32[]{:S(2)}, u32[]{:S(2)}) async-start(f32[16,64,512]{2,1,0:T(8,128)} %bitcast.21), calls=%async_computation.1 | async-start | bytes 4194304 | tf_op jit(solution)/shard_map/all_to_all | solution.py:62
  43.2 35.6 %collective-permute-start.2 = (f32[512,768]{1,0:T(8,128)S(1)}, f32[512,768]{1,0:T(8,128)S(1)}, u32[]{:S(2)}, u32[]{:S(2)}) collective-permute-start(f32[512,768]{1,0:T(8,128)S(1)} %get-tuple-element.42), channel_id=1, source_target_pairs={{0,1},{1,0},{2,3},{3,2},{4,5},{5,4},{6,7},{7,6},{8,9},{9,8},{10,11... | collective-permute-start | bytes 4718600 | tf_op jit(solution)/shard_map/ppermute | solution.py:54
  88.6 77.9 %all-to-all-start.2 = ((f32[16,64,768]{2,1,0:T(8,128)}), f32[16,64,768]{2,1,0:T(8,128)S(1)}, u32[]{:S(2)}, u32[]{:S(2)}) async-start(f32[16,64,768]{2,1,0:T(8,128)} %bitcast.19), calls=%async_computation.2 | async-start | bytes 6291456 | tf_op jit(solution)/shard_map/all_to_all | solution.py:62
  96.3 58.1 %collective-permute-start.1 = (f32[512,1280]{1,0:T(8,128)S(1)}, f32[512,1280]{1,0:T(8,128)S(1)}, u32[]{:S(2)}, u32[]{:S(2)}) collective-permute-start(f32[512,1280]{1,0:T(8,128)S(1)} %get-tuple-element.44), channel_id=1, source_target_pairs={{0,1},{1,0},{2,3},{3,2},{4,5},{5,4},{6,7},{7,6},{8,9},{9,8},{10,11... | collective-permute-start | bytes 7864328 | tf_op jit(solution)/shard_map/ppermute | solution.py:54
  166.5 151.4 %all-to-all-start.3 = ((f32[16,64,1280]{2,1,0:T(8,128)}), f32[16,64,1280]{2,1,0:T(8,128)}, u32[]{:S(2)}, u32[]{:S(2)}) async-start(f32[16,64,1280]{2,1,0:T(8,128)} %bitcast.18), calls=%async_computation.3 | async-start | bytes 10485760 | tf_op jit(solution)/shard_map/all_to_all | solution.py:62
  180.5 114.3 %collective-permute-start = (f32[512,2560]{1,0:T(8,128)S(1)}, f32[512,2560]{1,0:T(8,128)}, u32[]{:S(2)}, u32[]{:S(2)}) collective-permute-start(f32[512,2560]{1,0:T(8,128)S(1)} %get-tuple-element.38), channel_id=1, source_target_pairs={{0,1},{1,0},{2,3},{3,2},{4,5},{5,4},{6,7},{7,6},{8,9},{9,8},{10,11... | collective-permute-start | bytes 15728648 | tf_op jit(solution)/shard_map/ppermute | solution.py:54
  317.9 234.2 %all-to-all-start.4 = ((f32[16,64,2560]{2,1,0:T(8,128)}), f32[16,64,2560]{2,1,0:T(8,128)}, u32[]{:S(2)}, u32[]{:S(2)}) async-start(f32[16,64,2560]{2,1,0:T(8,128)} %bitcast.16), calls=%async_computation.4 | async-start | bytes 20971520 | tf_op jit(solution)/shard_map/all_to_all | solution.py:62
  328.9 91.9 %collective-permute-start.5 = (f32[512,2048]{1,0:T(8,128)S(1)}, f32[512,2048]{1,0:T(8,128)S(1)}, u32[]{:S(2)}, u32[]{:S(2)}) collective-permute-start(f32[512,2048]{1,0:T(8,128)S(1)} %get-tuple-element.36), channel_id=1, source_target_pairs={{0,1},{1,0},{2,3},{3,2},{4,5},{5,4},{6,7},{7,6},{8,9},{9,8},{10,11... | collective-permute-start | bytes 12582920 | tf_op jit(solution)/shard_map/ppermute | solution.py:54
  420.8 2.0 copy-start.2
  552.1 187.1 %all-to-all-start.5 = ((f32[16,64,2048]{2,1,0:T(8,128)}), f32[16,64,2048]{2,1,0:T(8,128)}, u32[]{:S(2)}, u32[]{:S(2)}) async-start(f32[16,64,2048]{2,1,0:T(8,128)} %bitcast.17), calls=%async_computation.5 | async-start | bytes 16777216 | tf_op jit(solution)/shard_map/all_to_all | solution.py:62
  560.0 26.1 %collective-permute-start.6 = (f32[512,512]{1,0:T(8,128)}, f32[512,512]{1,0:T(8,128)}, u32[]{:S(2)}, u32[]{:S(2)}) collective-permute-start(f32[512,512]{1,0:T(8,128)} %get-tuple-element.34), channel_id=1, source_target_pairs={{0,1},{1,0},{2,3},{3,2},{4,5},{5,4},{6,7},{7,6},{8,9},{9,8},{10,11... | collective-permute-start | bytes 3145736 | tf_op jit(solution)/shard_map/ppermute | solution.py:54
  580.3 4.4 collective-permute-start.4
  617.5 14.4 %copy-start.1 = (f32[1024,768]{1,0:T(8,128)S(1)}, f32[1024,768]{1,0:T(8,128)}, u32[]{:S(2)}) copy-start(f32[1024,768]{1,0:T(8,128)} %gather_fusion.7) | copy-start | bytes 9437188
  739.2 52.2 %all-to-all-start.6 = ((f32[16,64,512]{2,1,0:T(8,128)}), f32[16,64,512]{2,1,0:T(8,128)S(1)}, u32[]{:S(2)}, u32[]{:S(2)}) async-start(f32[16,64,512]{2,1,0:T(8,128)} %bitcast.20), calls=%async_computation.6 | async-start | bytes 4194304 | tf_op jit(solution)/shard_map/all_to_all | solution.py:62
